TPU v7x, 32 devices: a whole 2x2x4 slice. The times are simulated.
32 devices in a mesh: row: 4 (over y, x), col: 8 (over z, core).
Axes of the slice: x: 2, y: 2, z: 4, core: 2. Of those that a mesh axis runs over, the one named last changes fastest.
Arguments:
- features: bfloat16 [131072, 256], P(('row', 'col')), may hold values from -6 to 6
- send_rows: int32 [32, 32, 128], P(('row', 'col')), may hold values from 0 to 4095
- counts: int32 [32, 32], P(('row', 'col')), may hold values from 112 to 128, as said below
- tile_dst: int32 [32, 64], P(('row', 'col')), may hold values from 0 to 31
- tile_src: int32 [32, 64], P(('row', 'col')), may hold values from 0 to 63, each once within a row
- tiles: int32 [32, 64, 128, 128], P(('row', 'col')), may hold values 0 or 1
- w_self: bfloat16 [256, 256], replicated, may hold values from -0.375 to 0.375
- w_neigh: bfloat16 [256, 256], replicated, may hold values from -1.5 to 1.5
- bias: float32 [256], replicated, may hold values from -1 to 1
- cotangent: bfloat16 [131072, 256], P(('row', 'col')), may hold values from -6 to 6
Outputs:
- layer_out: bfloat16 [131072, 256], P(('row', 'col'))
- grad_features: float32 [131072, 256], P(('row', 'col'))
- grad_self: float32 [256, 256], replicated
- grad_neigh: float32 [256, 256], replicated
- grad_bias: float32 [256], replicated
Inputs may be any that keep to these rules, and one draw needn't show every extreme that they name: Every partition p has some q with counts[p, q] = 128.
All inputs are finite; a program needn't handle non-finite values. No bound on the sum of `tiles` on one device may be relied on, other than what follows from the above.
Results may differ from a plain program's by a relative error of at most 0.0051.
Values may be sent and summed in bfloat16 or wider, within the bound.
No kernel may reach another device: no remote copies, remote signals or barrier semaphores. Data moves between devices by JAX's collectives and lax.ppermute only.
A program may use at most 192 MiB of HBM per device.

v0:
```python
import jax
import jax.numpy as jnp
from jax import lax
from jax.sharding import PartitionSpec as P


def move_rows(block):
    return lax.all_to_all(block, ("row", "col"), split_axis=0, concat_axis=0, tiled=True)


def move_grads(block):
    return lax.all_to_all(block, ("row", "col"), split_axis=0, concat_axis=0, tiled=True)


def on_device(
    features, send_rows, counts, tile_dst, tile_src, tiles, w_self, w_neigh, bias, cotangent
):
    rows_own, width = features.shape
    peers = send_rows.shape[1]
    tile_rows = send_rows.shape[2]
    own_blocks = rows_own // tile_rows
    src_blocks = own_blocks + peers
    picks = send_rows[0]
    slots = jnp.arange(tile_rows, dtype=jnp.int32)
    keep = (slots[None, :] < counts[0][:, None]).reshape(-1)
    flat_picks = picks.reshape(-1)
    outgoing = jnp.take(features, flat_picks, axis=0) * keep[:, None].astype(jnp.bfloat16)
    arrived = move_rows(outgoing.reshape(peers, tile_rows, width))
    source = jnp.concatenate([features, arrived.reshape(peers * tile_rows, width)], 0)
    source = source.reshape(src_blocks, tile_rows, width)
    dst = tile_dst[0]
    src = tile_src[0]
    adj_int = tiles[0]
    adj = adj_int.astype(jnp.bfloat16)
    picked = jnp.take(source, src, axis=0)
    prod = jnp.einsum("tij,tjf->tif", adj, picked, preferred_element_type=jnp.float32)
    neigh = jax.ops.segment_sum(prod, dst, num_segments=own_blocks).reshape(rows_own, width)
    degree = jax.ops.segment_sum(
        jnp.sum(adj_int, axis=2).astype(jnp.float32), dst, num_segments=own_blocks
    ).reshape(rows_own)
    scale = 1.0 / (1.0 + degree)
    agg = (neigh * scale[:, None]).astype(jnp.bfloat16)
    pre = (
        jnp.dot(features, w_self, preferred_element_type=jnp.float32)
        + jnp.dot(agg, w_neigh, preferred_element_type=jnp.float32)
        + bias
    )
    sig = jax.nn.sigmoid(pre)
    layer_out = (pre * sig).astype(jnp.bfloat16)
    dpre = cotangent.astype(jnp.float32) * (sig * (1.0 + pre * (1.0 - sig)))
    dpre_b = dpre.astype(jnp.bfloat16)
    term_self = lax.dot_general(
        features, dpre_b, (((0,), (0,)), ((), ())), preferred_element_type=jnp.float32
    )
    term_neigh = lax.dot_general(
        agg, dpre_b, (((0,), (0,)), ((), ())), preferred_element_type=jnp.float32
    )
    term_bias = jnp.sum(dpre, axis=0)
    g_rows = lax.dot_general(
        dpre_b, w_neigh, (((1,), (1,)), ((), ())), preferred_element_type=jnp.float32
    )
    g_rows = (g_rows * scale[:, None]).astype(jnp.bfloat16)
    g_blocks = jnp.take(g_rows.reshape(own_blocks, tile_rows, width), dst, axis=0)
    back = jnp.einsum("tij,tif->tjf", adj, g_blocks, preferred_element_type=jnp.float32)
    back_sum = jax.ops.segment_sum(back, src, num_segments=src_blocks).reshape(
        src_blocks * tile_rows, width
    )
    back_b = back_sum[rows_own:].astype(jnp.bfloat16)
    returned = move_grads(back_b.reshape(peers, tile_rows, width))
    returned = returned.reshape(peers * tile_rows, width).astype(jnp.float32) * keep[
        :, None
    ].astype(jnp.float32)
    self_grad = lax.dot_general(
        dpre_b, w_self, (((1,), (1,)), ((), ())), preferred_element_type=jnp.float32
    )
    grad_features = (
        self_grad
        + back_sum[:rows_own]
        + jax.ops.segment_sum(returned, flat_picks, num_segments=rows_own)
    )
    total_self, total_neigh, total_bias = lax.psum(
        (term_self, term_neigh, term_bias), ("row", "col")
    )
    inv_root = 1.0 / jnp.sqrt(jnp.float32(rows_own * lax.axis_size(("row", "col"))))
    return (
        layer_out,
        grad_features,
        total_self * inv_root,
        total_neigh * inv_root,
        total_bias * inv_root,
    )


def solution(mesh):
    in_specs = (
        P(("row", "col"), None),
        P(("row", "col"), None, None),
        P(("row", "col"), None),
        P(("row", "col"), None),
        P(("row", "col"), None),
        P(("row", "col"), None, None, None),
        P(),
        P(),
        P(),
        P(("row", "col"), None),
    )
    out_specs = (P(("row", "col"), None), P(("row", "col"), None), P(), P(), P())
    return jax.shard_map(
        on_device, mesh=mesh, in_specs=in_specs, out_specs=out_specs, check_vma=False
    )
```

profile of v0, /device:TPU:0, one launch (start us, length us, event | category | flops | bytes accessed | tf_op | source)
XLA Modules:
  0.0 379.2 jit_solution(15681713276999709895)
XLA Ops:
  7.2 0.0 copy-start
  7.2 0.8 compare_select_fusion
  8.0 0.8 convert_bitcast_fusion
  8.8 14.9 %gather_fusion = bf16[4096,256]{1,0:T(8,128)(2,1)S(1)} fusion(bf16[4096,256]{1,0:T(8,128)(2,1)} %param.10, s32[4096]{0:T(1024)S(1)} %broadcast_clamp_fusion), kind=kCustom, calls=%fused_computation | custom fusion | bytes 4210688 | tf_op jit(solution)/shard_map/jit(_take)/gather | solution.py:27
  23.6 2.6 select_multiply_fusion
  26.3 7.5 %all-to-all-start = ((bf16[32,128,256]{2,1,0:T(8,128)(2,1)}), bf16[32,128,256]{2,1,0:T(8,128)(2,1)}, u32[]{:S(2)}, u32[]{:S(2)}) async-start(bf16[32,128,256]{2,1,0:T(8,128)(2,1)} %select_multiply_fusion), calls=%async_computation | async-start | bytes 4194304 | tf_op jit(solution)/shard_map/all_to_all | solution.py:8
  33.8 3.3 reduce_sum.18
  37.1 0.0 copy-done.9
  37.1 1.0 scatter_custom_fusion.1
  38.1 0.0 copy-done.10
  38.2 0.0 copy-done.2
  38.2 0.0 copy-done.8
  38.2 2.7 fusion.32
  40.9 42.8 %all-to-all-done = bf16[32,128,256]{2,1,0:T(8,128)(2,1)} async-done(((bf16[32,128,256]{2,1,0:T(8,128)(2,1)}), bf16[32,128,256]{2,1,0:T(8,128)(2,1)}, u32[]{:S(2)}, u32[]{:S(2)}) %all-to-all-start) | async-done | bytes 2097184 | tf_op jit(solution)/shard_map/all_to_all | solution.py:8
  83.8 3.8 %pad_maximum_fusion = bf16[8192,256]{1,0:T(8,128)(2,1)} fusion(bf16[4096,256]{1,0:T(8,128)(2,1)} %bitcast.7, bf16[4096,256]{1,0:T(8,128)(2,1)S(1)} %copy-done.2), kind=kLoop, calls=%fused_computation.13 | loop fusion | flops 8388608 | bytes 8388608 | tf_op jit(solution)/shard_map/concatenate | solution.py:29
  87.6 5.0 %gather_fusion.1 = bf16[64,128,256]{2,1,0:T(8,128)(2,1)} fusion(bf16[64,128,256]{2,1,0:T(8,128)(2,1)} %bitcast.59, s32[1024]{0:T(1024)S(1)} %pad_clamp_fusion.1), kind=kCustom, calls=%fused_computation.1 | custom fusion | bytes 8388864 | tf_op jit(solution)/shard_map/jit(_take)/gather | solution.py:35
  92.5 8.2 %fusion.10 = f32[64,128,256]{1,2,0:T(8,128)} fusion(bf16[64,128,256]{2,1,0:T(8,128)(2,1)} %gather_fusion.1, pred[64]{0:T(512)(128)(4,1)S(1)} %compare_and_fusion.2, s32[1,64,128,128]{3,2,1,0:T(8,128)} %param.15), kind=kOutput, calls=%fused_computation.27 | convolution fusion | flops 540016640 | bytes 16777280 | tf_op jit(solution)/shard_map/tij,tjf->tif/dot_general | solution.py:36
  100.7 9.0 %copy.21 = f32[64,128,256]{2,1,0:T(8,128)} copy(f32[64,128,256]{1,2,0:T(8,128)} %fusion.10) | data formatting | bytes 16777216 | tf_op jit(solution)/shard_map/tij,tjf->tif/dot_general | solution.py:36
  109.7 2.5 broadcast_in_dim.40
  112.2 19.4 %scatter_fusion = f32[32,128,256]{2,1,0:T(8,128)} fusion(f32[32,128,256]{2,1,0:T(8,128)} %broadcast_in_dim.40, s32[64]{0:T(128)S(1)} %bitcast.67, f32[64,128,256]{2,1,0:T(8,128)} %copy.21), kind=kCustom, calls=%fused_computation.3 | custom fusion | flops 2097152 | bytes 25166080 | tf_op jit(solution)/shard_map/scatter-add | solution.py:37
  131.5 2.7 fusion.3
  134.3 0.7 copy-done.3
  135.0 0.7 copy-done.11
  135.7 3.4 fusion.31
  139.1 1.3 copy-done.4
  140.4 2.0 fusion.1
  142.4 4.4 %gather_fusion.2 = bf16[64,128,256]{2,1,0:T(8,128)(2,1)} fusion(bf16[32,128,256]{2,1,0:T(8,128)(2,1)} %bitcast.58, s32[1024]{0:T(1024)S(1)} %pad_clamp_fusion), kind=kCustom, calls=%fused_computation.2 | custom fusion | bytes 8388864 | tf_op jit(solution)/shard_map/jit(_take)/gather | solution.py:63
  146.8 8.2 %fusion.13 = f32[64,128,256]{1,2,0:T(8,128)} fusion(bf16[64,128,256]{2,1,0:T(8,128)(2,1)} %gather_fusion.2, pred[64]{0:T(512)(128)(4,1)S(1)} %compare_and_fusion.1, s32[1,64,128,128]{3,2,1,0:T(8,128)} %param.15), kind=kOutput, calls=%fused_computation.28 | convolution fusion | flops 540016640 | bytes 16777280 | tf_op jit(solution)/shard_map/tij,tif->tjf/dot_general | solution.py:64
  155.0 9.0 %copy.23 = f32[64,128,256]{2,1,0:T(8,128)} copy(f32[64,128,256]{1,2,0:T(8,128)} %fusion.13) | data formatting | bytes 16777216 | tf_op jit(solution)/shard_map/tij,tif->tjf/dot_general | solution.py:64
  164.0 4.2 %broadcast_in_dim.45 = f32[64,128,256]{2,1,0:T(8,128)} broadcast(f32[]{:T(128)} %constant.24.clone.1), dimensions={} | broadcast | bytes 8388612 | tf_op jit(solution)/shard_map/broadcast_in_dim | solution.py:65
  168.3 19.8 %scatter_fusion.1 = f32[64,128,256]{2,1,0:T(8,128)} fusion(f32[64,128,256]{2,1,0:T(8,128)} %broadcast_in_dim.45, s32[64]{0:T(128)S(1)} %bitcast.68, f32[64,128,256]{2,1,0:T(8,128)} %copy.23), kind=kCustom, calls=%fused_computation.5 | custom fusion | flops 2097152 | bytes 25166080 | tf_op jit(solution)/shard_map/scatter-add | solution.py:65
  188.1 3.8 slice.23
  191.9 3.5 all-to-all-start.1
  195.3 0.3 all-reduce.3.cloned.1.call-start
  195.6 4.8 %slice.20 = f32[32,128,256]{2,1,0:T(8,128)} slice(f32[64,128,256]{2,1,0:T(8,128)} %scatter_fusion.1), slice={[0:32], [0:128], [0:256]} | slice | bytes 8388608 | tf_op jit(solution)/shard_map/slice | solution.py:78
  200.4 1.6 fusion.33
  202.1 1.4 convolution_bitcast_fusion
  203.5 0.0 all-reduce.3.cloned.1.call-update
  203.5 5.6 %convolution_add_fusion = f32[4096,256]{1,0:T(8,128)} fusion(f32[4096,256]{1,0:T(8,128)} %bitcast.60, bf16[4096,256]{1,0:T(8,128)(2,1)} %copy-done.4, bf16[256,256]{1,0:T(8,128)(2,1)S(1)} %copy-done.8), kind=kOutput, calls=%fused_computation.8 | convolution fusion | flops 537919488 | bytes 10616832 | tf_op jit(solution)/shard_map/dot_general | solution.py:73
  209.1 57.6 %psum.23 = f32[256]{0:T(256)S(1)} all-reduce(f32[256]{0:T(256)S(1)} %get-tuple-element.17), channel_id=1, replica_groups=mesh['row'=4,'col'=8] {'row','col'}, use_global_device_ids=true, to_apply=%region_8.9 | all-reduce | flops 256 | bytes 2048 | tf_op jit(solution)/shard_map/psum | solution.py:81
  266.7 0.6 broadcast_multiply_fusion.2
  267.3 72.4 %all-reduce.3.cloned.1.call-done = (f32[256,256]{0,1:T(8,128)}, f32[256,256]{0,1:T(8,128)}) async-done(((f32[256,256]{0,1:T(8,128)}, f32[256,256]{0,1:T(8,128)}), (f32[256,256]{0,1:T(8,128)}, f32[256,256]{0,1:T(8,128)})) %all-reduce.3.cloned.1.call-update) | async-done | bytes 524304 | tf_op jit(solution)/shard_map/psum | solution.py:81
  339.6 1.0 broadcast_multiply_fusion.1
  340.6 0.8 copy.25
  341.5 1.0 broadcast_multiply_fusion
  342.5 0.8 copy.26
  343.3 0.0 all-to-all-done.1
  343.3 29.0 %scatter_custom_fusion.3 = f32[4096,256]{1,0:T(8,128)} fusion(f32[4096,256]{1,0:T(8,128)} %convolution_add_fusion, s32[4096]{0:T(1024)} %bitcast.64, bf16[4096,256]{1,0:T(8,128)(2,1)} %bitcast.24, f32[4096]{0:T(1024)S(1)} %get-tuple-element.20), kind=kCustom, calls=%fused_computation.15 | custom fusion | flops 3145728 | bytes 6307840 | tf_op jit(solution)/shard_map/scatter-add | solution.py:79
  (26 shorter events, 0.1 us)
Async XLA Ops:
  7.2 127.1 %copy-start = (bf16[256,256]{1,0:T(8,128)(2,1)S(1)}, bf16[256,256]{1,0:T(8,128)(2,1)}, u32[]{:S(2)}) copy-start(bf16[256,256]{1,0:T(8,128)(2,1)} %param.17) | copy-start | bytes 393220
  26.3 10.8 %copy-start.9 = (s32[1,64]{1,0:T(1,128)S(1)}, s32[1,64]{1,0:T(1,128)}, u32[]{:S(2)}) copy-start(s32[1,64]{1,0:T(1,128)} %param.13) | copy-start | bytes 772
  26.3 11.8 %copy-start.10 = (s32[1,64]{1,0:T(1,128)S(1)}, s32[1,64]{1,0:T(1,128)}, u32[]{:S(2)}) copy-start(s32[1,64]{1,0:T(1,128)} %param.14) | copy-start | bytes 772
  26.3 11.9 %copy-start.2 = (bf16[4096,256]{1,0:T(8,128)(2,1)S(1)}, bf16[4096,256]{1,0:T(8,128)(2,1)}, u32[]{:S(2)}) copy-start(bf16[4096,256]{1,0:T(8,128)(2,1)} %param.10) | copy-start | bytes 6291460
  26.3 11.9 %copy-start.8 = (bf16[256,256]{1,0:T(8,128)(2,1)S(1)}, bf16[256,256]{1,0:T(8,128)(2,1)}, u32[]{:S(2)}) copy-start(bf16[256,256]{1,0:T(8,128)(2,1)} %param.16) | copy-start | bytes 393220
  26.3 57.5 %all-to-all-start = ((bf16[32,128,256]{2,1,0:T(8,128)(2,1)}), bf16[32,128,256]{2,1,0:T(8,128)(2,1)}, u32[]{:S(2)}, u32[]{:S(2)}) async-start(bf16[32,128,256]{2,1,0:T(8,128)(2,1)} %select_multiply_fusion), calls=%async_computation | async-start | bytes 4194304 | tf_op jit(solution)/shard_map/all_to_all | solution.py:8
  131.5 3.4 copy-start.3
  131.5 4.1 %copy-start.11 = (bf16[4096,256]{1,0:T(8,128)(2,1)S(1)}, bf16[4096,256]{1,0:T(8,128)(2,1)}, u32[]{:S(2)}) copy-start(bf16[4096,256]{1,0:T(8,128)(2,1)} %param.19) | copy-start | bytes 6291460
  131.5 4.1 %copy-start.12 = (f32[256]{0:T(256)S(1)}, f32[256]{0:T(256)}, u32[]{:S(2)}) copy-start(f32[256]{0:T(256)} %param.18) | copy-start | bytes 3076
  135.7 3.4 copy-start.6
  139.1 1.3 copy-start.4
  191.9 151.4 %all-to-all-start.1 = ((bf16[32,128,256]{2,1,0:T(8,128)(2,1)}), bf16[32,128,256]{2,1,0:T(8,128)(2,1)}, u32[]{:S(2)}, u32[]{:S(2)}) async-start(bf16[32,128,256]{2,1,0:T(8,128)(2,1)} %slice.23), calls=%async_computation.1 | async-start | bytes 4194304 | tf_op jit(solution)/shard_map/all_to_all | solution.py:12
  195.3 144.3 %all-reduce.3.cloned.1.call-start = ((), (), s32[]{:S(2)}) async-start(), calls=%async_computation.2 | async-start | bytes 1048576 | tf_op jit(solution)/shard_map/psum | solution.py:81
  195.6 4.8 %copy-start.5 = (bf16[4096,256]{1,0:T(8,128)(2,1)S(1)}, bf16[4096,256]{1,0:T(8,128)(2,1)}, u32[]{:S(2)}) copy-start(bf16[4096,256]{1,0:T(8,128)(2,1)} %copy-done.4) | copy-start | bytes 6291460
  195.6 4.8 %copy-start.7 = (bf16[4096,256]{1,0:T(8,128)(2,1)S(1)}, bf16[4096,256]{1,0:T(8,128)(2,1)}, u32[]{:S(2)}) copy-start(bf16[4096,256]{1,0:T(8,128)(2,1)} %copy-done.6) | copy-start | bytes 6291460
  339.6 32.7 %copy-start.1 = (bf16[256,256]{1,0:T(8,128)(2,1)S(1)}, bf16[256,256]{1,0:T(8,128)(2,1)}, u32[]{:S(2)}) copy-start(bf16[256,256]{1,0:T(8,128)(2,1)} %param.17) | copy-start | bytes 393220
Sparse Core Ops, SparseCore 0:
  203.7 135.9 all-reduce.2
where the time goes:
time: 380 us; the launch traced here: 379 us
  waiting for transfers between devices  115 us (30%)
  other arithmetic  85.8 us (23%)
  local copies, waits for them, and re-layouts  62 us (16%)
  blocking collectives  57.6 us (15%)
  matrix products  33.2 us (9%)
  between operations  14.2 us (4%)
  starting transfers between devices  11.2 us (3%)
    psum x1, waiting for transfers between devices, on_device(): lax.psum((term_self, term_neigh, term_bias), ('row', 'col'))  72.4 us
    psum x1, blocking collectives, on_device(): lax.psum((term_self, term_neigh, term_bias), ('row', 'col'))  57.6 us
    all_to_all x1, waiting for transfers between devices, move_rows(): lax.all_to_all(block, ('row', 'col'), split_axis=0, concat_axis=0, tiled=...  42.8 us
    scatter-add x1, other arithmetic, on_device(): jax.ops.segment_sum(returned, flat_picks, num_segments=rows_own)  29 us
    scatter-add x1, other arithmetic, on_device(): jax.ops.segment_sum(back, src, num_segments=src_blocks)  19.8 us
    scatter-add x1, other arithmetic, on_device(): jax.ops.segment_sum(prod, dst, num_segments=own_blocks)  19.4 us
    gather x1, local copies, waits for them, and re-layouts, on_device(): jnp.take(features, flat_picks, axis=0) * keep[:, None].astype(jnp.bfloat16)  14.9 us
    dot_general x1, local copies, waits for them, and re-layouts, on_device(): jnp.einsum('tij,tjf->tif', adj, picked, preferred_element_type=jnp.float32)  9 us
  transfers between devices with their start and end apart: 3, of which 2 were waited for; matrix products, arithmetic and copies ran while one was open for 7% of the time, Pallas kernels for 0%

commit v1 on v0

--- a/solution.py
+++ b/solution.py
@@ -79,7 +79,7 @@
         + jax.ops.segment_sum(returned, flat_picks, num_segments=rows_own)
     )
     total_self, total_neigh, total_bias = lax.psum(
-        (term_self, term_neigh, term_bias), ("row", "col")
+        lax.psum((term_self, term_neigh, term_bias), "col"), "row"
     )
     inv_root = 1.0 / jnp.sqrt(jnp.float32(rows_own * lax.axis_size(("row", "col"))))
     return (

time: 380 us -> 356 us (0.937)
  waiting for transfers between devices: 115 us -> 95.7 us
    psum x1 -> x2, waiting for transfers between devices: 72.4 us -> 52.9 us  [the longest x1 41.3 us: on_device(): lax.psum(lax.psum((term_self, term_neigh, term_bias), 'col'), 'row')]
    psum x1 -> x2, blocking collectives: 57.6 us -> 55.4 us  [the longest x1 45 us: on_device(): lax.psum((term_self, term_neigh, term_bias), 'col')]
  transfers between devices with their start and end apart: 3 -> 4, of which waited for: 2 -> 3; matrix products, arithmetic and copies ran while one was open for 7% -> 6% of each run, Pallas kernels for 0% -> 0%
where the time goes in v1:
time: 356 us; the launch traced here: 355 us
  waiting for transfers between devices  95.7 us (27%)
  other arithmetic  85.8 us (24%)
  local copies, waits for them, and re-layouts  60 us (17%)
  blocking collectives  55.4 us (16%)
  matrix products  32.7 us (9%)
  between operations  14.2 us (4%)
  starting transfers between devices  11.2 us (3%)
    psum x1, blocking collectives, on_device(): lax.psum((term_self, term_neigh, term_bias), 'col')  45 us
    all_to_all x1, waiting for transfers between devices, move_rows(): lax.all_to_all(block, ('row', 'col'), split_axis=0, concat_axis=0, tiled=...  42.8 us
    psum x1, waiting for transfers between devices, on_device(): lax.psum(lax.psum((term_self, term_neigh, term_bias), 'col'), 'row')  41.3 us
    scatter-add x1, other arithmetic, on_device(): jax.ops.segment_sum(returned, flat_picks, num_segments=rows_own)  29 us
    scatter-add x1, other arithmetic, on_device(): jax.ops.segment_sum(back, src, num_segments=src_blocks)  19.8 us
    scatter-add x1, other arithmetic, on_device(): jax.ops.segment_sum(prod, dst, num_segments=own_blocks)  19.3 us
    gather x1, local copies, waits for them, and re-layouts, on_device(): jnp.take(features, flat_picks, axis=0) * keep[:, None].astype(jnp.bfloat16)  14.9 us
    psum x1, waiting for transfers between devices, on_device(): lax.psum((term_self, term_neigh, term_bias), 'col')  11.6 us
  transfers between devices with their start and end apart: 4, of which 3 were waited for; matrix products, arithmetic and copies ran while one was open for 6% of the time, Pallas kernels for 0%

profile of v1, /device:TPU:0, one launch (start us, length us, event | category | flops | bytes accessed | tf_op | source)
XLA Modules:
  0.0 355.1 jit_solution(8511312299684732988)
XLA Ops:
  7.2 0.0 copy-start
  7.2 0.8 compare_select_fusion
  8.0 0.8 convert_bitcast_fusion
  8.8 14.9 %gather_fusion = bf16[4096,256]{1,0:T(8,128)(2,1)S(1)} fusion(bf16[4096,256]{1,0:T(8,128)(2,1)} %param.10, s32[4096]{0:T(1024)S(1)} %broadcast_clamp_fusion), kind=kCustom, calls=%fused_computation | custom fusion | bytes 4210688 | tf_op jit(solution)/shard_map/jit(_take)/gather | solution.py:27
  23.6 2.6 select_multiply_fusion
  26.3 7.5 %all-to-all-start = ((bf16[32,128,256]{2,1,0:T(8,128)(2,1)}), bf16[32,128,256]{2,1,0:T(8,128)(2,1)}, u32[]{:S(2)}, u32[]{:S(2)}) async-start(bf16[32,128,256]{2,1,0:T(8,128)(2,1)} %select_multiply_fusion), calls=%async_computation | async-start | bytes 4194304 | tf_op jit(solution)/shard_map/all_to_all | solution.py:8
  33.8 3.3 reduce_sum.18
  37.1 1.0 scatter_custom_fusion.1
  38.2 2.7 fusion.32
  40.9 42.8 %all-to-all-done = bf16[32,128,256]{2,1,0:T(8,128)(2,1)} async-done(((bf16[32,128,256]{2,1,0:T(8,128)(2,1)}), bf16[32,128,256]{2,1,0:T(8,128)(2,1)}, u32[]{:S(2)}, u32[]{:S(2)}) %all-to-all-start) | async-done | bytes 2097184 | tf_op jit(solution)/shard_map/all_to_all | solution.py:8
  83.8 3.8 %pad_maximum_fusion = bf16[8192,256]{1,0:T(8,128)(2,1)} fusion(bf16[4096,256]{1,0:T(8,128)(2,1)} %bitcast.7, bf16[4096,256]{1,0:T(8,128)(2,1)S(1)} %copy-done.2), kind=kLoop, calls=%fused_computation.13 | loop fusion | flops 8388608 | bytes 8388608 | tf_op jit(solution)/shard_map/concatenate | solution.py:29
  87.5 5.0 %gather_fusion.1 = bf16[64,128,256]{2,1,0:T(8,128)(2,1)} fusion(bf16[64,128,256]{2,1,0:T(8,128)(2,1)} %bitcast.59, s32[1024]{0:T(1024)S(1)} %pad_clamp_fusion.1), kind=kCustom, calls=%fused_computation.1 | custom fusion | bytes 8388864 | tf_op jit(solution)/shard_map/jit(_take)/gather | solution.py:35
  92.5 8.2 %fusion.10 = f32[64,128,256]{1,2,0:T(8,128)} fusion(bf16[64,128,256]{2,1,0:T(8,128)(2,1)} %gather_fusion.1, pred[64]{0:T(512)(128)(4,1)S(1)} %compare_and_fusion.2, s32[1,64,128,128]{3,2,1,0:T(8,128)} %param.15), kind=kOutput, calls=%fused_computation.27 | convolution fusion | flops 540016640 | bytes 16777280 | tf_op jit(solution)/shard_map/tij,tjf->tif/dot_general | solution.py:36
  100.7 9.0 %copy.21 = f32[64,128,256]{2,1,0:T(8,128)} copy(f32[64,128,256]{1,2,0:T(8,128)} %fusion.10) | data formatting | bytes 16777216 | tf_op jit(solution)/shard_map/tij,tjf->tif/dot_general | solution.py:36
  109.7 2.5 broadcast_in_dim.40
  112.2 19.3 %scatter_fusion = f32[32,128,256]{2,1,0:T(8,128)} fusion(f32[32,128,256]{2,1,0:T(8,128)} %broadcast_in_dim.40, s32[64]{0:T(128)S(1)} %bitcast.67, f32[64,128,256]{2,1,0:T(8,128)} %copy.21), kind=kCustom, calls=%fused_computation.3 | custom fusion | flops 2097152 | bytes 25166080 | tf_op jit(solution)/shard_map/scatter-add | solution.py:37
  131.5 2.7 fusion.3
  134.3 0.7 copy-done.3
  134.9 0.7 copy-done.11
  135.6 3.4 fusion.31
  139.0 1.3 copy-done.4
  140.4 2.0 fusion.1
  142.4 4.4 %gather_fusion.2 = bf16[64,128,256]{2,1,0:T(8,128)(2,1)} fusion(bf16[32,128,256]{2,1,0:T(8,128)(2,1)} %bitcast.58, s32[1024]{0:T(1024)S(1)} %pad_clamp_fusion), kind=kCustom, calls=%fused_computation.2 | custom fusion | bytes 8388864 | tf_op jit(solution)/shard_map/jit(_take)/gather | solution.py:63
  146.8 8.2 %fusion.13 = f32[64,128,256]{1,2,0:T(8,128)} fusion(bf16[64,128,256]{2,1,0:T(8,128)(2,1)} %gather_fusion.2, pred[64]{0:T(512)(128)(4,1)S(1)} %compare_and_fusion.1, s32[1,64,128,128]{3,2,1,0:T(8,128)} %param.15), kind=kOutput, calls=%fused_computation.28 | convolution fusion | flops 540016640 | bytes 16777280 | tf_op jit(solution)/shard_map/tij,tif->tjf/dot_general | solution.py:64
  155.0 9.0 %copy.23 = f32[64,128,256]{2,1,0:T(8,128)} copy(f32[64,128,256]{1,2,0:T(8,128)} %fusion.13) | data formatting | bytes 16777216 | tf_op jit(solution)/shard_map/tij,tif->tjf/dot_general | solution.py:64
  164.0 4.2 %broadcast_in_dim.45 = f32[64,128,256]{2,1,0:T(8,128)} broadcast(f32[]{:T(128)} %constant.24.clone.1), dimensions={} | broadcast | bytes 8388612 | tf_op jit(solution)/shard_map/broadcast_in_dim | solution.py:65
  168.2 19.8 %scatter_fusion.1 = f32[64,128,256]{2,1,0:T(8,128)} fusion(f32[64,128,256]{2,1,0:T(8,128)} %broadcast_in_dim.45, s32[64]{0:T(128)S(1)} %bitcast.68, f32[64,128,256]{2,1,0:T(8,128)} %copy.23), kind=kCustom, calls=%fused_computation.5 | custom fusion | flops 2097152 | bytes 25166080 | tf_op jit(solution)/shard_map/scatter-add | solution.py:65
  188.0 3.8 %slice.23 = bf16[32,128,256]{2,1,0:T(8,128)(2,1)} slice(f32[64,128,256]{2,1,0:T(8,128)} %scatter_fusion.1), slice={[32:64], [0:128], [0:256]} | slice | bytes 4194304 | tf_op jit(solution)/shard_map/slice | solution.py:68
  191.8 3.5 all-to-all-start.1
  195.3 0.3 all-reduce.5.cloned.1.call-start
  195.6 4.0 %fusion.33 = f32[256,256]{0,1:T(8,128)} fusion(bf16[4096,256]{1,0:T(8,128)(2,1)} %copy-done.7, bf16[4096,256]{1,0:T(8,128)(2,1)} %copy-done.4), kind=kOutput, calls=%fused_computation.66 | convolution fusion | flops 536870912 | bytes 4456448 | tf_op jit(solution)/shard_map/dot_general | solution.py:55
  199.6 1.5 convolution_bitcast_fusion
  201.1 0.0 all-reduce.5.cloned.1.call-update
  201.1 0.0 all-reduce.7.cloned.1.call-start
  201.1 45.0 %psum.46 = f32[256]{0:T(256)S(1)} all-reduce(f32[256]{0:T(256)S(1)} %get-tuple-element.19), channel_id=1, replica_groups=mesh['row'=4,'col'=8] {'col'}, use_global_device_ids=true, to_apply=%region_10.11 | all-reduce | flops 256 | bytes 2048 | tf_op jit(solution)/shard_map/psum | solution.py:82
  246.1 10.4 %psum.47 = f32[256]{0:T(256)S(1)} all-reduce(f32[256]{0:T(256)S(1)} %psum.46), channel_id=1, replica_groups=mesh['row'=4,'col'=8] {'row'}, use_global_device_ids=true, to_apply=%region_11.12 | all-reduce | flops 256 | bytes 2048 | tf_op jit(solution)/shard_map/psum | solution.py:81
  256.5 11.6 %all-reduce.5.cloned.1.call-done = (f32[256,256]{0,1:T(8,128)}, f32[256,256]{0,1:T(8,128)}) async-done(((f32[256,256]{0,1:T(8,128)}, f32[256,256]{0,1:T(8,128)}), (f32[256,256]{0,1:T(8,128)}, f32[256,256]{0,1:T(8,128)})) %all-reduce.5.cloned.1.call-update) | async-done | bytes 524304 | tf_op jit(solution)/shard_map/psum | solution.py:82
  268.1 0.0 all-reduce.7.cloned.1.call-update
  268.1 0.6 broadcast_multiply_fusion.2
  268.7 2.7 slice.20
  271.4 0.2 copy-done.6
  271.6 2.8 convolution_add_fusion
  274.3 41.3 %all-reduce.7.cloned.1.call-done = (f32[256,256]{0,1:T(8,128)}, f32[256,256]{0,1:T(8,128)}) async-done(((f32[256,256]{0,1:T(8,128)}, f32[256,256]{0,1:T(8,128)}), (f32[256,256]{0,1:T(8,128)}, f32[256,256]{0,1:T(8,128)})) %all-reduce.7.cloned.1.call-update) | async-done | bytes 524304 | tf_op jit(solution)/shard_map/psum | solution.py:81
  315.6 1.0 broadcast_multiply_fusion.1
  316.6 0.8 copy.25
  317.4 1.0 broadcast_multiply_fusion
  318.4 0.8 copy.26
  319.3 29.0 %scatter_custom_fusion.3 = f32[4096,256]{1,0:T(8,128)} fusion(f32[4096,256]{1,0:T(8,128)} %convolution_add_fusion, s32[4096]{0:T(1024)} %bitcast.64, bf16[4096,256]{1,0:T(8,128)(2,1)} %bitcast.24, f32[4096]{0:T(1024)S(1)} %get-tuple-element.22), kind=kCustom, calls=%fused_computation.15 | custom fusion | flops 3145728 | bytes 6307840 | tf_op jit(solution)/shard_map/scatter-add | solution.py:79
  (30 shorter events, 0.1 us)
Async XLA Ops:
  7.2 127.1 %copy-start = (bf16[256,256]{1,0:T(8,128)(2,1)S(1)}, bf16[256,256]{1,0:T(8,128)(2,1)}, u32[]{:S(2)}) copy-start(bf16[256,256]{1,0:T(8,128)(2,1)} %param.17) | copy-start | bytes 393220
  26.3 10.8 %copy-start.9 = (s32[1,64]{1,0:T(1,128)S(1)}, s32[1,64]{1,0:T(1,128)}, u32[]{:S(2)}) copy-start(s32[1,64]{1,0:T(1,128)} %param.13) | copy-start | bytes 772
  26.3 11.8 %copy-start.10 = (s32[1,64]{1,0:T(1,128)S(1)}, s32[1,64]{1,0:T(1,128)}, u32[]{:S(2)}) copy-start(s32[1,64]{1,0:T(1,128)} %param.14) | copy-start | bytes 772
  26.3 11.9 %copy-start.2 = (bf16[4096,256]{1,0:T(8,128)(2,1)S(1)}, bf16[4096,256]{1,0:T(8,128)(2,1)}, u32[]{:S(2)}) copy-start(bf16[4096,256]{1,0:T(8,128)(2,1)} %param.10) | copy-start | bytes 6291460
  26.3 11.9 %copy-start.8 = (bf16[256,256]{1,0:T(8,128)(2,1)S(1)}, bf16[256,256]{1,0:T(8,128)(2,1)}, u32[]{:S(2)}) copy-start(bf16[256,256]{1,0:T(8,128)(2,1)} %param.16) | copy-start | bytes 393220
  26.3 57.5 %all-to-all-start = ((bf16[32,128,256]{2,1,0:T(8,128)(2,1)}), bf16[32,128,256]{2,1,0:T(8,128)(2,1)}, u32[]{:S(2)}, u32[]{:S(2)}) async-start(bf16[32,128,256]{2,1,0:T(8,128)(2,1)} %select_multiply_fusion), calls=%async_computation | async-start | bytes 4194304 | tf_op jit(solution)/shard_map/all_to_all | solution.py:8
  131.5 3.4 copy-start.3
  131.5 4.1 %copy-start.11 = (bf16[4096,256]{1,0:T(8,128)(2,1)S(1)}, bf16[4096,256]{1,0:T(8,128)(2,1)}, u32[]{:S(2)}) copy-start(bf16[4096,256]{1,0:T(8,128)(2,1)} %param.19) | copy-start | bytes 6291460
  131.5 4.1 %copy-start.12 = (f32[256]{0:T(256)S(1)}, f32[256]{0:T(256)}, u32[]{:S(2)}) copy-start(f32[256]{0:T(256)} %param.18) | copy-start | bytes 3076
  135.6 3.4 copy-start.7
  139.0 1.4 copy-start.4
  191.8 127.4 %all-to-all-start.1 = ((bf16[32,128,256]{2,1,0:T(8,128)(2,1)}), bf16[32,128,256]{2,1,0:T(8,128)(2,1)}, u32[]{:S(2)}, u32[]{:S(2)}) async-start(bf16[32,128,256]{2,1,0:T(8,128)(2,1)} %slice.23), calls=%async_computation.1 | async-start | bytes 4194304 | tf_op jit(solution)/shard_map/all_to_all | solution.py:12
  195.3 72.8 %all-reduce.5.cloned.1.call-start = ((), (), s32[]{:S(2)}) async-start(), calls=%async_computation.2 | async-start | bytes 1048576 | tf_op jit(solution)/shard_map/psum | solution.py:82
  195.6 4.0 %copy-start.5 = (bf16[4096,256]{1,0:T(8,128)(2,1)S(1)}, bf16[4096,256]{1,0:T(8,128)(2,1)}, u32[]{:S(2)}) copy-start(bf16[4096,256]{1,0:T(8,128)(2,1)} %copy-done.4) | copy-start | bytes 6291460
  201.1 114.5 %all-reduce.7.cloned.1.call-start = ((), (), s32[]{:S(2)}) async-start(), calls=%async_computation.3 | async-start | bytes 1048576 | tf_op jit(solution)/shard_map/psum | solution.py:81
  268.7 2.9 copy-start.6
  315.6 32.7 %copy-start.1 = (bf16[256,256]{1,0:T(8,128)(2,1)S(1)}, bf16[256,256]{1,0:T(8,128)(2,1)}, u32[]{:S(2)}) copy-start(bf16[256,256]{1,0:T(8,128)(2,1)} %param.17) | copy-start | bytes 393220
Sparse Core Ops, SparseCore 0:
  201.2 66.8 all-reduce.4
  271.1 44.4 all-reduce.6
